TPU v7x, 512 devices: a 8x2x16 block of a 8x8x16 slice. The times are simulated.
512 devices in a mesh: grp: 2 (over y), seq: 128 (over z, x), head: 2 (over core).
Axes of the slice: x: 8, y: 2, z: 16, core: 2. Of those that a mesh axis runs over, the one named last changes fastest.
The devices are a block of a 8x8x16 slice.
Arguments:
- key_cache: bfloat16 [4, 1024, 128, 1024], P('grp', ('seq', 'head')), parts along dimension 0, may hold values from -160 to 160, as said below
- value_cache: bfloat16 [4, 1024, 128, 1024], P('grp', ('seq', 'head')), parts along dimension 0, may hold values from -16 to 16, as said below
- query: bfloat16 [4, 4096], P('grp', 'head'), parts along dimension 0, may hold values from -48 to 48, as said below
- lengths: int32 [4], P('grp'), parts along dimension 0, may hold values from 128 to 131072, as said below
- block_map: int32 [4, 1024], P('grp'), parts along dimension 0, may hold values from 0 to 1023, each once within a row
Outputs:
- attended: bfloat16 [4, 4096], P('grp', 'head'), parts along dimension 0
There are 2 independent parts, one for each index of `grp`. A program takes and returns all parts, laid end to end along the dimension named above; each array names one. Nothing has to cross between parts.
Inputs may be any that keep to these rules, and one draw needn't show every extreme that they name: `lengths`: every length is a multiple of 128; in every draw some request has length 131072. `key_cache`: finite entries, drawn afresh for every request, block, token and channel. `value_cache`: finite entries, drawn afresh for every request, block, token and channel. `query`: finite entries, drawn afresh for every request, head and channel.
All inputs are finite; a program needn't handle non-finite values.
Results may differ from a plain program's by a relative error of at most 0.0055.
Values may be sent and summed in bfloat16 or wider, within the bound.
No kernel may reach another device: no remote copies, remote signals or barrier semaphores. Data moves between devices by JAX's collectives and lax.ppermute only.
A program may use at most 64 MiB of HBM per device.

v0:
```python
import jax
import jax.numpy as jnp
from jax import lax
from jax.sharding import Mesh
from jax.sharding import PartitionSpec as P

QH = 32
KVH = 8
HD = 128
BLK = 128
SEQ = ("seq_0", "seq_1")
SEQ_HEAD = ("seq_0", "seq_1", "head")


def all_in_one(shard, axis):
    leaves = jax.tree.leaves(shard)
    sequence = sorted(range(len(leaves)), key=lambda k: -leaves[k].size)
    width = (1, *leaves[sequence[0]].shape)[-1]
    lines = [
        jnp.pad(leaves[k].reshape(-1), (0, -leaves[k].size % width)).reshape(-1, width)
        for k in sequence
    ]
    both, at, found = (lax.all_gather(jnp.concatenate(lines), axis), 0, {})
    for k, line in zip(sequence, lines):
        share = both[:, at : at + len(line)].reshape(len(both), -1)
        found[k] = share[:, : leaves[k].size].reshape(-1, *leaves[k].shape)
        at += len(line)
    numbers = iter(range(len(leaves)))
    return jax.tree.map(lambda _: found[next(numbers)], shard)


def combined_by_axis(shard, axes, combine):
    for axis in axes:
        pieces = all_in_one(shard, axis)
        shard = jax.tree.map(lambda part: part[0], pieces)
        for k in range(1, lax.axis_size(axis)):
            shard = combine(shard, jax.tree.map(lambda part: part[k], pieces))
    return shard


def combine(earlier, later):
    top_new = jnp.maximum(earlier[0], later[0])
    factor_a = jnp.exp(earlier[0] - top_new)
    factor_b = jnp.exp(later[0] - top_new)
    total = earlier[1] * factor_a + later[1] * factor_b
    summed_values = earlier[2] * factor_a[..., None] + later[2] * factor_b[..., None]
    return (top_new, total, summed_values)


def partials(key_rows, value_rows, queries, live_blocks):
    batch_rows = key_rows.shape[0]
    slot_count = key_rows.shape[1]
    group_count = key_rows.shape[3] // HD
    token_count = slot_count * BLK
    key_flat = key_rows.reshape(batch_rows, token_count, group_count, HD)
    value_flat = value_rows.reshape(batch_rows, token_count, group_count, HD)
    query_heads = queries.reshape(batch_rows, group_count, QH // KVH, HD)
    logit_scores = jnp.einsum(
        "bgqd,btgd->bgqt", query_heads, key_flat, preferred_element_type=jnp.float32
    )
    logit_scores = logit_scores * (1.0 / HD**0.5)
    logit_scores = logit_scores.reshape(batch_rows, group_count, QH // KVH, slot_count, BLK)
    live_mask = live_blocks[:, None, None, :, None]
    row_top = jnp.max(jnp.where(live_mask, logit_scores, jnp.float32(-1e30)), axis=(3, 4))
    expo = jnp.where(live_mask, jnp.exp(logit_scores - row_top[..., None, None]), jnp.float32(0.0))
    total = jnp.sum(expo, axis=(3, 4))
    weights = expo.astype(jnp.bfloat16).reshape(batch_rows, group_count, QH // KVH, token_count)
    summed_values = jnp.einsum(
        "bgqt,btgd->bgqd", weights, value_flat, preferred_element_type=jnp.float32
    )
    return (row_top, total, summed_values)


def owned_live(block_map, lengths, position, count):
    owned_blocks = lax.dynamic_slice_in_dim(block_map, position * count, count, 1)
    return owned_blocks < (lengths // BLK)[:, None]


def on_device(key_cache, value_cache, query, lengths, block_map):
    batch_rows = key_cache.shape[0]
    width_here = query.shape[1]
    key_rows, value_rows = (
        lax.all_to_all(key_cache, "head", split_axis=3, concat_axis=1, tiled=True),
        lax.all_to_all(value_cache, "head", split_axis=3, concat_axis=1, tiled=True),
    )
    live_blocks = owned_live(block_map, lengths, lax.axis_index(SEQ), key_rows.shape[1])
    local = partials(key_rows, value_rows, query, live_blocks)
    row_top, total, summed_values = combined_by_axis(local, SEQ, combine)
    result = summed_values / total[..., None]
    return result.reshape(batch_rows, width_here).astype(jnp.bfloat16)


def solution(mesh):
    torus = Mesh(
        mesh.devices.reshape(mesh.shape["grp"], 16, 8, mesh.shape["head"]),
        ("grp", "seq_0", "seq_1", "head"),
    )
    placed = (
        P("grp", SEQ_HEAD, None, None),
        P("grp", SEQ_HEAD, None, None),
        P("grp", "head"),
        P("grp"),
        P("grp", None),
    )
    return jax.shard_map(
        on_device, mesh=torus, in_specs=placed, out_specs=P("grp", "head"), check_vma=False
    )
```

profile of v0, /device:TPU:80, one launch (start us, length us, event | category | flops | bytes accessed | tf_op | source)
XLA Modules:
  0.0 132.9 jit_solution(2421228417511749975)
XLA Ops:
  0.0 4.3 %copy.10 = bf16[2,4,128,1024]{2,1,0,3:T(4,128)(2,1)} copy(bf16[2,4,128,1024]{3,2,1,0:T(8,128)(2,1)} %param.5) | data formatting | bytes 4194304 | tf_op args[0]
  4.3 3.9 %all-to-all-start = ((bf16[2,4,128,1024]{2,1,0,3:T(4,128)(2,1)}), bf16[2,4,128,1024]{2,1,0,3:T(4,128)(2,1)S(1)}, u32[]{:S(2)}, u32[]{:S(2)}) async-start(bf16[2,4,128,1024]{2,1,0,3:T(4,128)(2,1)} %copy.10), calls=%async_computation | async-start | bytes 4194304 | tf_op jit(solution)/shard_map/all_to_all | solution.py:83
  8.3 0.8 dynamic-slice_compare_fusion
  9.2 4.3 %copy.13 = bf16[2,4,128,1024]{2,1,0,3:T(4,128)(2,1)} copy(bf16[2,4,128,1024]{3,2,1,0:T(8,128)(2,1)} %param.6) | data formatting | bytes 4194304 | tf_op args[1]
  13.5 4.8 %all-to-all-start.1 = ((bf16[2,4,128,1024]{2,1,0,3:T(4,128)(2,1)}), bf16[2,4,128,1024]{2,1,0,3:T(4,128)(2,1)}, u32[]{:S(2)}, u32[]{:S(2)}) async-start(bf16[2,4,128,1024]{2,1,0,3:T(4,128)(2,1)} %copy.13), calls=%async_computation.1 | async-start | bytes 4194304 | tf_op jit(solution)/shard_map/all_to_all | solution.py:84
  18.3 3.0 %copy.11 = bf16[2,4,128,2,512]{4,2,1,3,0:T(8,128)(2,1)} copy(bf16[2,4,128,2,512]{2,1,0,4,3:T(4,128)(2,1)S(1)} %bitcast.574) | data formatting | bytes 4194304 | tf_op jit(solution)/shard_map/all_to_all | solution.py:83
  21.4 2.5 %reshape.1675 = bf16[2,1024,4,128]{3,2,1,0:T(4,128)(2,1)S(1)} reshape(bf16[2,2,4,128,512]{4,3,2,1,0:T(8,128)(2,1)} %bitcast.575) | data formatting | bytes 4194304 | tf_op jit(solution)/shard_map/reshape | solution.py:55
  23.9 0.7 select_reduce_fusion
  24.7 0.2 fusion.7
  25.0 3.0 %copy.14 = bf16[2,4,128,2,512]{4,2,1,3,0:T(8,128)(2,1)S(1)} copy(bf16[2,4,128,2,512]{2,1,0,4,3:T(4,128)(2,1)} %bitcast.2) | data formatting | bytes 4194304 | tf_op jit(solution)/shard_map/all_to_all | solution.py:84
  28.0 2.1 %reshape.1676 = bf16[2,1024,4,128]{3,2,1,0:T(4,128)(2,1)} reshape(bf16[2,2,4,128,512]{4,3,2,1,0:T(8,128)(2,1)S(1)} %bitcast.576) | data formatting | bytes 4194304 | tf_op jit(solution)/shard_map/reshape | solution.py:56
  30.1 2.1 %fusion = f32[2,4,4,128]{3,2,1,0:T(4,128)S(1)} fusion(bf16[2,1024,4,128]{3,2,1,0:T(4,128)(2,1)} %reshape.1676, f32[2,4,4,1024]{3,2,1,0:T(4,128)S(1)} %get-tuple-element.91, f32[2,4,4]{2,1,0:T(4,128)S(1)} %get-tuple-element.90, pred[2,1024]{1,0:T(4,128)(4,1)S(1)} %bitcast.619), kind=kOutput, calls=%fused_computation | convolution fusion | flops 8486912 | bytes 2246784 | tf_op jit(solution)/shard_map/bgqt,btgd->bgqd/dot_general | solution.py:68
  32.2 69.8 %all-gather.2 = f32[16,34,128]{2,1,0:T(8,128)S(1)} all-gather(f32[1,34,128]{2,1,0:T(8,128)S(1)} %maximum_bitcast_fusion), channel_id=2, replica_groups=mesh['grp'=2,'seq_0'=16,'seq_1'=8,'head'=2] {'seq_0'}, dimensions={0}, use_global_device_ids=true | all-gather | bytes 295936 | tf_op jit(solution)/shard_map/all_gather | solution.py:23
  102.2 0.2 fusion.14
  102.4 26.6 %all-gather.3 = f32[8,34,128]{2,1,0:T(8,128)S(1)} all-gather(f32[1,34,128]{2,1,0:T(8,128)S(1)} %maximum_bitcast_fusion.1), channel_id=3, replica_groups=mesh['grp'=2,'seq_0'=16,'seq_1'=8,'head'=2] {'seq_1'}, dimensions={0}, use_global_device_ids=true | all-gather | bytes 156672 | tf_op jit(solution)/shard_map/all_gather | solution.py:23
  129.5 0.1 squeeze.268
  129.6 0.1 squeeze.266
  129.7 0.1 squeeze.265
  129.8 0.1 squeeze.278
  129.9 0.1 squeeze.287
  130.0 0.1 squeeze.286
  130.1 0.1 squeeze.285
  130.2 0.1 squeeze.283
  132.2 0.7 fusion.58
  (72 shorter events, 2.8 us)
Async XLA Ops:
  4.3 3.9 %copy-start.1 = (s32[2]{0:T(128)S(1)}, s32[2]{0:T(128)}, u32[]{:S(2)}) copy-start(s32[2]{0:T(128)} %param.8) | copy-start | bytes 28
  4.3 4.8 %copy-start = (bf16[2,2048]{1,0:T(2,128)(2,1)S(1)}, bf16[2,2048]{1,0:T(2,128)(2,1)}, u32[]{:S(2)}) copy-start(bf16[2,2048]{1,0:T(2,128)(2,1)} %param.7) | copy-start | bytes 24580
  4.3 9.1 %all-to-all-start = ((bf16[2,4,128,1024]{2,1,0,3:T(4,128)(2,1)}), bf16[2,4,128,1024]{2,1,0,3:T(4,128)(2,1)S(1)}, u32[]{:S(2)}, u32[]{:S(2)}) async-start(bf16[2,4,128,1024]{2,1,0,3:T(4,128)(2,1)} %copy.10), calls=%async_computation | async-start | bytes 4194304 | tf_op jit(solution)/shard_map/all_to_all | solution.py:83
  13.5 11.6 %all-to-all-start.1 = ((bf16[2,4,128,1024]{2,1,0,3:T(4,128)(2,1)}), bf16[2,4,128,1024]{2,1,0,3:T(4,128)(2,1)}, u32[]{:S(2)}, u32[]{:S(2)}) async-start(bf16[2,4,128,1024]{2,1,0,3:T(4,128)(2,1)} %copy.13), calls=%async_computation.1 | async-start | bytes 4194304 | tf_op jit(solution)/shard_map/all_to_all | solution.py:84
where the time goes:
time: 133 us
  blocking collectives  96.4 us (72%)
  local copies, waits for them, and re-layouts  22.6 us (17%)
  starting transfers between devices  8.77 us (7%)
  matrix products  2.8 us (2%)
  other arithmetic  2.06 us (2%)
    all_gather x2, blocking collectives, all_in_one(): both, at, found = (lax.all_gather(jnp.concatenate(lines), axis), 0, {})  96.4 us
    unnamed x8, local copies, waits for them, and re-layouts  8.7 us
    all_to_all x1, starting transfers between devices, on_device(): lax.all_to_all(value_cache, 'head', split_axis=3, concat_axis=1, tiled=True)  4.84 us
    all_to_all x1, starting transfers between devices, on_device(): lax.all_to_all(key_cache, 'head', split_axis=3, concat_axis=1, tiled=True)  3.92 us
    all_to_all x1, local copies, waits for them, and re-layouts, on_device(): lax.all_to_all(key_cache, 'head', split_axis=3, concat_axis=1, tiled=True)  3.04 us
    all_to_all x1, local copies, waits for them, and re-layouts, on_device(): lax.all_to_all(value_cache, 'head', split_axis=3, concat_axis=1, tiled=True)  2.98 us
  transfers between devices with their start and end apart: 2, of which 0 were waited for; matrix products, arithmetic and copies ran while one was open for 9% of the time, Pallas kernels for 0%

commit v1 on v0

--- a/solution.py
+++ b/solution.py
@@ -79,9 +79,18 @@
 def on_device(key_cache, value_cache, query, lengths, block_map):
     batch_rows = key_cache.shape[0]
     width_here = query.shape[1]
+
+    def work_tables(mat, link_axis, d0, ndim_at):
+        return jnp.concatenate(
+            lax.all_to_all(
+                jnp.stack(jnp.split(mat, lax.psum(1, link_axis), axis=d0), axis=0), link_axis, 0, 0
+            ),
+            axis=ndim_at,
+        )
+
     key_rows, value_rows = (
         lax.all_to_all(key_cache, "head", split_axis=3, concat_axis=1, tiled=True),
-        lax.all_to_all(value_cache, "head", split_axis=3, concat_axis=1, tiled=True),
+        work_tables(value_cache, "head", d0=3, ndim_at=1),
     )
     live_blocks = owned_live(block_map, lengths, lax.axis_index(SEQ), key_rows.shape[1])
     local = partials(key_rows, value_rows, query, live_blocks)

time: 133 us -> 131 us (0.985)
  local copies, waits for them, and re-layouts: 22.6 us -> 18.8 us
  other arithmetic: 2.06 us -> 3.6 us
    unnamed x8 -> x7, local copies, waits for them, and re-layouts: 8.7 us -> 4.4 us
    another operation x0 -> x2, local copies, waits for them, and re-layouts: none -> 3.83 us  [the longest x1 2.09 us: partials(): value_flat = value_rows.reshape(batch_rows, token_count, group_count, HD)]
    all_to_all x1 -> x0, local copies, waits for them, and re-layouts: 2.98 us -> none  [on_device(): lax.all_to_all(value_cache, 'head', split_axis=3, concat_axis=1, tiled=True)]
    another operation x0 -> x1, other arithmetic: none -> 1.54 us  [work_tables(): jnp.stack(jnp.split(mat, lax.psum(1, link_axis), axis=d0), axis=0)]
  transfers between devices with their start and end apart: 2 -> 2, of which waited for: 0 -> 0; matrix products, arithmetic and copies ran while one was open for 9% -> 8% of each run, Pallas kernels for 0% -> 0%
where the time goes in v1:
time: 131 us
  blocking collectives  96.4 us (74%)
  local copies, waits for them, and re-layouts  18.8 us (14%)
  starting transfers between devices  8.77 us (7%)
  other arithmetic  3.6 us (3%)
  matrix products  2.8 us (2%)
    all_gather x2, blocking collectives, all_in_one(): both, at, found = (lax.all_gather(jnp.concatenate(lines), axis), 0, {})  96.4 us
    all_to_all x1, starting transfers between devices, work_tables(): lax.all_to_all(jnp.stack(jnp.split(mat, lax.psum(1, link_axis), axis=d0),...  4.84 us
    unnamed x7, local copies, waits for them, and re-layouts  4.4 us
    all_to_all x1, starting transfers between devices, on_device(): lax.all_to_all(key_cache, 'head', split_axis=3, concat_axis=1, tiled=True)  3.92 us
    all_to_all x1, local copies, waits for them, and re-layouts, on_device(): lax.all_to_all(key_cache, 'head', split_axis=3, concat_axis=1, tiled=True)  3.04 us
  transfers between devices with their start and end apart: 2, of which 0 were waited for; matrix products, arithmetic and copies ran while one was open for 8% of the time, Pallas kernels for 0%

profile of v1, /device:TPU:80, one launch (start us, length us, event | category | flops | bytes accessed | tf_op | source)
XLA Modules:
  0.0 130.7 jit_solution(3574117170436312253)
XLA Ops:
  0.0 4.3 %copy.10 = bf16[2,4,128,1024]{2,1,0,3:T(4,128)(2,1)} copy(bf16[2,4,128,1024]{3,2,1,0:T(8,128)(2,1)} %param.5) | data formatting | bytes 4194304 | tf_op args[0]
  4.3 3.9 %all-to-all-start = ((bf16[2,4,128,1024]{2,1,0,3:T(4,128)(2,1)}), bf16[2,4,128,1024]{2,1,0,3:T(4,128)(2,1)S(1)}, u32[]{:S(2)}, u32[]{:S(2)}) async-start(bf16[2,4,128,1024]{2,1,0,3:T(4,128)(2,1)} %copy.10), calls=%async_computation | async-start | bytes 4194304 | tf_op jit(solution)/shard_map/all_to_all | solution.py:92
  8.3 0.8 dynamic-slice_compare_fusion
  9.2 1.7 %slice_bitcast_fusion.1 = (bf16[1,2,4,128,512]{4,3,2,1,0:T(8,128)(2,1)S(1)}, bf16[1,2,4,128,512]{4,3,2,1,0:T(8,128)(2,1)S(1)}) fusion(bf16[2,4,128,1024]{3,2,1,0:T(8,128)(2,1)} %param.6), kind=kLoop, calls=%fused_computation.7 | loop fusion | bytes 4194304 | tf_op jit(solution)/shard_map/stack | solution.py:86
  10.9 1.5 %pad_maximum_fusion = bf16[2,2,4,128,512]{4,3,2,1,0:T(8,128)(2,1)} fusion(bf16[1,2,4,128,512]{4,3,2,1,0:T(8,128)(2,1)S(1)} %get-tuple-element.79, bf16[1,2,4,128,512]{4,3,2,1,0:T(8,128)(2,1)S(1)} %get-tuple-element.78), kind=kLoop, calls=%fused_computation | loop fusion | flops 1048576 | bytes 4194304 | tf_op jit(solution)/shard_map/stack | solution.py:86
  12.4 4.8 %all-to-all-start.1 = ((bf16[2,2,4,128,512]{4,3,2,1,0:T(8,128)(2,1)}), bf16[2,2,4,128,512]{4,3,2,1,0:T(8,128)(2,1)}, u32[]{:S(2)}, u32[]{:S(2)}) async-start(bf16[2,2,4,128,512]{4,3,2,1,0:T(8,128)(2,1)} %pad_maximum_fusion), calls=%async_computation.1 | async-start | bytes 4194304 | tf_op jit(solution)/shard_map/all_to_all | solution.py:85
  17.3 3.0 %copy.11 = bf16[2,4,128,2,512]{4,2,1,3,0:T(8,128)(2,1)} copy(bf16[2,4,128,2,512]{2,1,0,4,3:T(4,128)(2,1)S(1)} %bitcast.577) | data formatting | bytes 4194304 | tf_op jit(solution)/shard_map/all_to_all | solution.py:92
  20.3 2.5 %reshape.1674 = bf16[2,1024,4,128]{3,2,1,0:T(4,128)(2,1)S(1)} reshape(bf16[2,2,4,128,512]{4,3,2,1,0:T(8,128)(2,1)} %bitcast.578) | data formatting | bytes 4194304 | tf_op jit(solution)/shard_map/reshape | solution.py:55
  22.9 0.7 select_reduce_fusion
  23.7 0.2 fusion.7
  24.0 1.8 %copy.13 = bf16[2,2,4,128,512]{4,3,2,1,0:T(8,128)(2,1)S(1)} copy(bf16[2,2,4,128,512]{4,3,2,0,1:T(8,128)(2,1)} %bitcast.4) | data formatting | bytes 4194304 | tf_op jit(solution)/shard_map/reshape | solution.py:84
  25.8 2.1 %reshape_reshape.2 = bf16[2,1024,4,128]{3,2,1,0:T(4,128)(2,1)} reshape(bf16[2,2,4,128,512]{4,3,2,1,0:T(8,128)(2,1)S(1)} %copy.13) | data formatting | bytes 4194304 | tf_op jit(solution)/shard_map/reshape;reshape | solution.py:56
  27.9 2.1 %fusion = f32[2,4,4,128]{3,2,1,0:T(4,128)S(1)} fusion(bf16[2,1024,4,128]{3,2,1,0:T(4,128)(2,1)} %reshape_reshape.2, f32[2,4,4,1024]{3,2,1,0:T(4,128)S(1)} %get-tuple-element.93, f32[2,4,4]{2,1,0:T(4,128)S(1)} %get-tuple-element.92, pred[2,1024]{1,0:T(4,128)(4,1)S(1)} %bitcast.616), kind=kOutput, calls=%fused_computation.1 | convolution fusion | flops 8486912 | bytes 2246784 | tf_op jit(solution)/shard_map/bgqt,btgd->bgqd/dot_general | solution.py:68
  30.0 69.8 %all-gather.2 = f32[16,34,128]{2,1,0:T(8,128)S(1)} all-gather(f32[1,34,128]{2,1,0:T(8,128)S(1)} %maximum_bitcast_fusion), channel_id=2, replica_groups=mesh['grp'=2,'seq_0'=16,'seq_1'=8,'head'=2] {'seq_0'}, dimensions={0}, use_global_device_ids=true | all-gather | bytes 295936 | tf_op jit(solution)/shard_map/all_gather | solution.py:23
  100.0 0.2 fusion.14
  100.2 26.6 %all-gather.3 = f32[8,34,128]{2,1,0:T(8,128)S(1)} all-gather(f32[1,34,128]{2,1,0:T(8,128)S(1)} %maximum_bitcast_fusion.1), channel_id=3, replica_groups=mesh['grp'=2,'seq_0'=16,'seq_1'=8,'head'=2] {'seq_1'}, dimensions={0}, use_global_device_ids=true | all-gather | bytes 156672 | tf_op jit(solution)/shard_map/all_gather | solution.py:23
  127.3 0.1 squeeze.268
  127.4 0.1 squeeze.266
  127.5 0.1 squeeze.265
  127.6 0.1 squeeze.278
  127.7 0.1 squeeze.287
  127.9 0.1 squeeze.284
  128.2 0.1 squeeze.281
  130.0 0.7 fusion.58
  (73 shorter events, 2.9 us)
Async XLA Ops:
  4.3 3.9 %copy-start.1 = (s32[2]{0:T(128)S(1)}, s32[2]{0:T(128)}, u32[]{:S(2)}) copy-start(s32[2]{0:T(128)} %param.8) | copy-start | bytes 28
  4.3 4.8 %copy-start = (bf16[2,2048]{1,0:T(2,128)(2,1)S(1)}, bf16[2,2048]{1,0:T(2,128)(2,1)}, u32[]{:S(2)}) copy-start(bf16[2,2048]{1,0:T(2,128)(2,1)} %param.7) | copy-start | bytes 24580
  4.3 8.1 %all-to-all-start = ((bf16[2,4,128,1024]{2,1,0,3:T(4,128)(2,1)}), bf16[2,4,128,1024]{2,1,0,3:T(4,128)(2,1)S(1)}, u32[]{:S(2)}, u32[]{:S(2)}) async-start(bf16[2,4,128,1024]{2,1,0,3:T(4,128)(2,1)} %copy.10), calls=%async_computation | async-start | bytes 4194304 | tf_op jit(solution)/shard_map/all_to_all | solution.py:92
  12.4 11.6 %all-to-all-start.1 = ((bf16[2,2,4,128,512]{4,3,2,1,0:T(8,128)(2,1)}), bf16[2,2,4,128,512]{4,3,2,1,0:T(8,128)(2,1)}, u32[]{:S(2)}, u32[]{:S(2)}) async-start(bf16[2,2,4,128,512]{4,3,2,1,0:T(8,128)(2,1)} %pad_maximum_fusion), calls=%async_computation.1 | async-start | bytes 4194304 | tf_op jit(solution)/shard_map/all_to_all | solution.py:85
